TPU v7x, 256 devices: a whole 4x4x8 slice. The times are simulated.
256 devices in a mesh: layer: 4 (over y), row: 8 (over x, z_lo), col: 8 (over z_hi, core).
Axes of the slice: x: 4, y: 4, z: 8 (z_hi: 4, z_lo: 2; z = z_hi * 2 + z_lo), core: 2. Of those that a mesh axis runs over, the one named last changes fastest.
Arguments:
- ancestor: float32 [8192, 8192], P('row', 'col'), may hold values from -768 to 3840, as said below
- coupling: bfloat16 [4, 8192, 1024], P('layer', ('row', 'col')), may hold values from -10 to 10
- fronts: float32 [4, 2, 512, 512], P('layer', None, None, ('row', 'col')), may hold values from -10 to 360, as said below
- tile_pattern: int32 [4, 2, 8], P('layer'), may hold values 0 or 1
Outputs:
- schur: float32 [8192, 8192], P('row', 'col')
- panel_factor: float32 [8192, 512], P(('row', 'col'))
- pivots: float32 [512], P(('row', 'col'))
Inputs may be any that keep to these rules, and one draw needn't show every extreme that they name: `ancestor`: symmetric and positive definite; the leading [512, 512] block of schur_0 stays positive definite after all layers' terms are subtracted. `fronts`: each [512, 512] block is symmetric and positive definite, with diagonal entries from 200 to 360 and other entries within -10 to 10.
All inputs are finite; a program needn't handle non-finite values. No bound on the sum of `tile_pattern` on one device may be relied on, other than what follows from the above.
Results may differ from a plain program's by a relative error of at most 0.0008.
Values may be sent and summed in bfloat16 or wider, within the bound.
A program may use at most 128 MiB of HBM per device.

v0:
```python
import jax
import jax.numpy as jnp
from jax import lax
from jax.sharding import PartitionSpec as P

S = 8192
TILE = 1024
P_SIZE = 512
NP = 2


def spread(value, axis, source):
    kept = jnp.where(lax.axis_index(axis) == source, value, 0).astype(value.dtype)
    return lax.psum(kept, axis)


def filled_up(lines, size):
    spare = -len(lines) % size
    return jnp.pad(lines, [(0, spare)] + [(0, 0)] * (lines.ndim - 1))


def spread_2(x, axis, root):
    lines = jnp.where(lax.axis_index(axis) == root, x, jnp.zeros_like(x)).reshape(
        -1, *x.shape[1:][-1:]
    )
    padded = filled_up(lines, lax.axis_size(axis))
    own = lax.psum_scatter(padded, axis, scatter_dimension=0, tiled=True)
    return lax.all_gather(own, axis, axis=0, tiled=True)[: len(lines)].reshape(x.shape)


def column_block(sender):
    row_count = lax.axis_size("row")
    col_count = lax.axis_size("col")
    col_place = lax.axis_index("col")
    first_root = col_place * row_count // col_count
    pieces = sender(first_root + 0)
    return pieces


def solve_rows(factor, columns):
    return lax.linalg.triangular_solve(
        factor, columns, left_side=False, lower=True, transpose_a=True
    )


def local(ancestor, coupling, fronts, tile_pattern):
    row_count = lax.axis_size("row")
    col_count = lax.axis_size("col")
    row_place = lax.axis_index("row")
    col_place = lax.axis_index("col")
    local_rows = S // (row_count * col_count)
    block_rows = S // row_count
    gathered = lax.all_gather(
        fronts.astype(jnp.bfloat16), ("row", "col"), axis=3, tiled=True
    ).astype(fronts.dtype)
    factors = jnp.linalg.cholesky(gathered[0])
    first_row = (row_place * col_count + col_place) * local_rows
    positions = first_row + lax.iota(jnp.int32, local_rows)
    onehot = (positions[:, None] // TILE == lax.iota(jnp.int32, S // TILE)[None, :]).astype(
        jnp.float32
    )
    row_masks = jnp.dot(onehot, tile_pattern[0].T.astype(jnp.float32))
    solved_parts = []
    for panel in range(NP):
        columns = (
            coupling[0, :, panel * P_SIZE : (panel + 1) * P_SIZE].astype(jnp.float32)
            * row_masks[:, panel : panel + 1]
        )
        solved_parts.append(solve_rows(factors[panel], columns))
    scaled = jnp.concatenate(solved_parts, 1).astype(jnp.bfloat16)
    row_side = lax.all_gather(scaled, "col", axis=0, tiled=True)
    col_side = column_block(lambda source: spread(row_side, "row", source))
    update = -lax.dot_general(
        row_side, col_side, (((1,), (1,)), ((), ())), preferred_element_type=jnp.float32
    )
    shared = lax.psum_scatter(
        update.astype(jnp.bfloat16), "layer", scatter_dimension=0, tiled=True
    ).astype(jnp.float32)
    summed = lax.all_gather(shared.astype(jnp.bfloat16), "layer", axis=0, tiled=True).astype(
        shared.dtype
    )
    leading = ancestor[:, :P_SIZE] + summed[:, :P_SIZE]
    global_rows = row_place * block_rows + lax.iota(jnp.int32, block_rows)
    trailing = None
    working = leading
    pivot_source = working[0:P_SIZE, 0:P_SIZE]
    pivot_block = spread(pivot_source, ("row", "col"), 0)
    pivot_chol = jnp.linalg.cholesky(pivot_block)
    keep_rows = (global_rows >= 0)[:, None]
    received = spread_2(working, "col", 0)
    solved = solve_rows(pivot_chol, received)
    panel_rows = jnp.where(keep_rows, solved, jnp.zeros_like(solved))
    panel_cols = column_block(lambda source: spread(panel_rows, "row", source))
    leading = leading - jnp.dot(
        panel_rows,
        panel_cols[:P_SIZE].T,
        precision=lax.Precision.HIGHEST,
        preferred_element_type=jnp.float32,
    )
    history = (panel_rows, panel_cols)
    panel_outs = lax.dynamic_slice_in_dim(panel_rows, col_place * local_rows, local_rows, 0)
    diagonal = jnp.diagonal(pivot_chol)
    pivot_outs = diagonal * diagonal
    trailing = ancestor[:, P_SIZE:] + summed[:, P_SIZE:]
    rows_part, cols_part = history
    trailing = trailing - jnp.dot(
        rows_part,
        cols_part[P_SIZE:].T,
        precision=lax.Precision.HIGHEST,
        preferred_element_type=jnp.float32,
    )
    schur = jnp.concatenate([leading, trailing], 1)
    pivot_share = pivot_outs.shape[0] // (row_count * col_count)
    flat_place = row_place * col_count + col_place
    my_pivots = lax.dynamic_slice_in_dim(pivot_outs, flat_place * pivot_share, pivot_share, 0)
    return (schur, panel_outs, my_pivots)


def solution(mesh):
    return jax.shard_map(
        local,
        mesh=mesh,
        in_specs=(
            P("row", "col"),
            P("layer", ("row", "col"), None),
            P("layer", None, None, ("row", "col")),
            P("layer", None, None),
        ),
        out_specs=(P("row", "col"), P(("row", "col"), None), P(("row", "col"))),
        check_vma=False,
    )
```

profile of v0, /device:TPU:1, one launch (start us, length us, event | category | flops | bytes accessed | tf_op | source)
XLA Modules:
  0.0 1092.7 jit_solution(2963737448343294521)
XLA Ops:
  12.0 115.7 %all-gather.5.cloned.1.call-done = bf16[1,2,512,512]{2,3,1,0:T(8,128)(2,1)} async-done(((bf16[1,2,512,8]{2,3,1,0:T(8,128)(2,1)}), bf16[1,2,512,512]{2,3,1,0:T(8,128)(2,1)}) %all-gather.5.cloned.1.call-update) | async-done | bytes 1048592 | tf_op jit(solution)/shard_map/all_gather | solution.py:53
  134.3 23.5 %custom-call.64 = f32[2,128,128]{2,1,0:T(8,128)S(1)} custom-call(f32[2,128,128]{2,1,0:T(8,128)S(1)} %cholesky.531), custom_call_target="Cholesky" | custom-call | tf_op jit(solution)/shard_map/jit(cholesky)/cholesky | solution.py:56
  157.8 19.7 %custom-call.65 = f32[2,1,128,128]{2,3,1,0:T(8,128)S(1)} custom-call(f32[2,1,128,128]{3,2,1,0:T(8,128)S(1)} %select_bitcast_fusion.2), custom_call_target="InvertDiagBlocksLowerTriangular" | custom-call | tf_op jit(solution)/shard_map/jit(cholesky)/cholesky | solution.py:56
  180.7 23.5 %custom-call.66 = f32[2,128,128]{2,1,0:T(8,128)S(1)} custom-call(f32[2,128,128]{2,1,0:T(8,128)S(1)} %cholesky.535), custom_call_target="Cholesky" | custom-call | tf_op jit(solution)/shard_map/jit(cholesky)/cholesky | solution.py:56
  204.2 19.8 %custom-call.67 = f32[2,1,128,128]{2,3,1,0:T(8,128)S(1)} custom-call(f32[2,1,128,128]{3,2,1,0:T(8,128)S(1)} %get-tuple-element.98), custom_call_target="InvertDiagBlocksLowerTriangular" | custom-call | tf_op jit(solution)/shard_map/jit(cholesky)/cholesky | solution.py:56
  226.1 23.5 %custom-call.68 = f32[2,128,128]{2,1,0:T(8,128)S(1)} custom-call(f32[2,128,128]{2,1,0:T(8,128)S(1)} %cholesky.540), custom_call_target="Cholesky" | custom-call | tf_op jit(solution)/shard_map/jit(cholesky)/cholesky | solution.py:56
  249.5 19.7 %custom-call.69 = f32[2,1,128,128]{2,3,1,0:T(8,128)S(1)} custom-call(f32[2,1,128,128]{3,2,1,0:T(8,128)S(1)} %get-tuple-element.96), custom_call_target="InvertDiagBlocksLowerTriangular" | custom-call | tf_op jit(solution)/shard_map/jit(cholesky)/cholesky | solution.py:56
  271.0 23.7 %custom-call.70 = f32[2,128,128]{2,1,0:T(8,128)S(1)} custom-call(f32[2,128,128]{2,1,0:T(8,128)S(1)} %convolution_subtract_fusion.7), custom_call_target="Cholesky" | custom-call | tf_op jit(solution)/shard_map/jit(cholesky)/cholesky | solution.py:56
  304.2 39.3 %custom-call.78 = f32[4,128,128]{1,2,0:T(8,128)S(1)} custom-call(f32[4,128,128]{2,1,0:T(8,128)S(1)} %get-tuple-element.26), custom_call_target="InvertDiagBlocksLowerTriangular" | custom-call | tf_op jit(solution)/shard_map/triangular_solve/custom-call.14 | solution.py:41
  352.1 39.7 %custom-call.79 = f32[4,128,128]{1,2,0:T(8,128)S(1)} custom-call(f32[4,128,128]{2,1,0:T(8,128)S(1)} %get-tuple-element.27), custom_call_target="InvertDiagBlocksLowerTriangular" | custom-call | tf_op jit(solution)/shard_map/triangular_solve/custom-call.14 | solution.py:41
  397.4 38.6 %all-gather.7.cloned.1.call-done = bf16[1024,1024]{0,1:T(8,128)(2,1)} async-done(((bf16[128,1024]{0,1:T(8,128)(2,1)}), bf16[1024,1024]{0,1:T(8,128)(2,1)}) %all-gather.7.cloned.1.call-update) | async-done | bytes 2097168 | tf_op jit(solution)/shard_map/all_gather | solution.py:71
  437.6 108.4 %all-reduce.6.cloned.1.call-done = bf16[1024,1024]{0,1:T(8,128)(2,1)} async-done(((bf16[1024,1024]{0,1:T(8,128)(2,1)}), bf16[1024,1024]{0,1:T(8,128)(2,1)}) %all-reduce.6.cloned.1.call-update) | async-done | bytes 2097168 | tf_op jit(solution)/shard_map/psum | solution.py:14
  551.4 32.3 %reduce-scatter.3.cloned.1.call-done = bf16[256,1024]{0,1:T(8,128)(2,1)} async-done(((bf16[1024,1024]{0,1:T(8,128)(2,1)}), bf16[256,1024]{0,1:T(8,128)(2,1)}) %reduce-scatter.3.cloned.1.call-update) | async-done | bytes 524304 | tf_op jit(solution)/shard_map/reduce_scatter | solution.py:76
  590.4 29.9 %all-gather.9.cloned.1.call-done = bf16[1024,1024]{0,1:T(8,128)(2,1)} async-done(((bf16[256,1024]{0,1:T(8,128)(2,1)}), bf16[1024,1024]{0,1:T(8,128)(2,1)}) %all-gather.9.cloned.1.call-update) | async-done | bytes 2097168 | tf_op jit(solution)/shard_map/all_gather | solution.py:79
  628.4 186.2 %all-reduce.8.cloned.1.call-done = f32[512,512]{0,1:T(8,128)} async-done(((f32[512,512]{0,1:T(8,128)}), f32[512,512]{0,1:T(8,128)}) %all-reduce.8.cloned.1.call-update) | async-done | bytes 1048592 | tf_op jit(solution)/shard_map/psum | solution.py:14
  816.5 11.7 %cholesky.467 = f32[128,128]{1,0:T(8,128)S(1)} custom-call(f32[128,128]{1,0:T(8,128)S(1)} %cholesky.544), custom_call_target="Cholesky" | custom-call | tf_op jit(solution)/shard_map/jit(cholesky)/cholesky | solution.py:88
  828.4 9.8 custom-call.71
  839.0 11.7 %cholesky.483 = f32[128,128]{1,0:T(8,128)S(1)} custom-call(f32[128,128]{1,0:T(8,128)S(1)} %cholesky.548), custom_call_target="Cholesky" | custom-call | tf_op jit(solution)/shard_map/jit(cholesky)/cholesky | solution.py:88
  850.8 10.0 custom-call.72
  862.0 11.7 %cholesky.504 = f32[128,128]{1,0:T(8,128)S(1)} custom-call(f32[128,128]{1,0:T(8,128)S(1)} %cholesky.553), custom_call_target="Cholesky" | custom-call | tf_op jit(solution)/shard_map/jit(cholesky)/cholesky | solution.py:88
  873.9 9.8 custom-call.73
  884.5 11.7 %cholesky.521 = f32[128,128]{1,0:T(8,128)S(1)} custom-call(f32[128,128]{1,0:T(8,128)S(1)} %convolution_subtract_fusion.12), custom_call_target="Cholesky" | custom-call | tf_op jit(solution)/shard_map/jit(cholesky)/cholesky | solution.py:88
  910.3 39.3 %custom-call.74 = f32[4,128,128]{1,2,0:T(8,128)S(1)} custom-call(f32[4,128,128]{2,1,0:T(8,128)S(1)} %get-tuple-element.19), custom_call_target="InvertDiagBlocksLowerTriangular" | custom-call | tf_op jit(solution)/shard_map/triangular_solve | solution.py:41
  968.1 99.3 %all-reduce.10.cloned.1.call-done = f32[1024,512]{0,1:T(8,128)} async-done(((f32[1024,512]{0,1:T(8,128)}), f32[1024,512]{0,1:T(8,128)}) %all-reduce.10.cloned.1.call-update) | async-done | bytes 2097168 | tf_op jit(solution)/shard_map/psum | solution.py:14
  (199 shorter events, 141.5 us)
Async XLA Ops:
  7.2 120.6 %all-gather.5.cloned.1.call-start = ((), (), s32[]{:S(2)}) async-start(), calls=%async_computation.2 | async-start | bytes 1064960 | tf_op jit(solution)/shard_map/all_gather | solution.py:53
  8.6 427.5 %all-gather.7.cloned.1.call-start = ((), (), s32[]{:S(2)}) async-start(), calls=%async_computation.3 | async-start | bytes 2359296 | tf_op jit(solution)/shard_map/all_gather | solution.py:71
  130.6 2.0 copy-start.5
  132.9 1.3 copy-start.4
  295.7 96.1 %copy-start.10 = (f32[128,512]{1,0:T(8,128)S(1)}, f32[128,512]{1,0:T(8,128)}, u32[]{:S(2)}) copy-start(f32[128,512]{1,0:T(8,128)} %get-tuple-element.93) | copy-start | bytes 786436
  295.7 98.5 %copy-start.9 = (f32[128,512]{1,0:T(8,128)S(1)}, f32[128,512]{1,0:T(8,128)}, u32[]{:S(2)}) copy-start(f32[128,512]{1,0:T(8,128)} %get-tuple-element.94) | copy-start | bytes 786436
  397.4 148.6 %all-reduce.6.cloned.1.call-start = ((), (), s32[]{:S(2)}) async-start(), calls=%async_computation.4 | async-start | bytes 4194304 | tf_op jit(solution)/shard_map/psum | solution.py:14
  437.5 108.5 %copy-start.8 = (bf16[1024,1024]{0,1:T(8,128)(2,1)S(1)}, bf16[1024,1024]{0,1:T(8,128)(2,1)}, u32[]{:S(2)}) copy-start(bf16[1024,1024]{0,1:T(8,128)(2,1)} %all-gather.7.cloned.1.call-done) | copy-start | bytes 6291460
  437.5 146.1 %reduce-scatter.3.cloned.1.call-start = ((), (), s32[]{:S(2)}) async-start(), calls=%async_computation.5 | async-start | bytes 2621440 | tf_op jit(solution)/shard_map/reduce_scatter | solution.py:76
  551.3 69.0 %all-gather.9.cloned.1.call-start = ((), (), s32[]{:S(2)}) async-start(), calls=%async_computation.6 | async-start | bytes 2621440 | tf_op jit(solution)/shard_map/all_gather | solution.py:79
  583.7 230.9 %all-reduce.8.cloned.1.call-start = ((), (), s32[]{:S(2)}) async-start(), calls=%async_computation.9 | async-start | bytes 2097152 | tf_op jit(solution)/shard_map/psum | solution.py:14
  622.4 2.7 copy-start
  625.0 1.3 copy-start.2
  627.4 233.9 %reduce-scatter.5.cloned.1.call-start = ((), (), s32[]{:S(2)}) async-start(), calls=%async_computation.7 | async-start | bytes 2359296 | tf_op jit(solution)/shard_map/reduce_scatter | solution.py:27
  628.2 321.5 %all-gather.11.cloned.1.call-start = ((), (), s32[]{:S(2)}) async-start(), calls=%async_computation.8 | async-start | bytes 2359296 | tf_op jit(solution)/shard_map/all_gather | solution.py:28
  814.6 1.7 copy-start.6
  861.4 206.1 %all-reduce.10.cloned.1.call-start = ((), (), s32[]{:S(2)}) async-start(), calls=%async_computation.10 | async-start | bytes 4194304 | tf_op jit(solution)/shard_map/psum | solution.py:14
  949.7 4.1 copy-start.7
  1067.5 5.7 copy-start.1
  1067.5 5.7 copy-start.3
Sparse Core Ops, SparseCore 0:
  10.4 117.2 all-gather.4
  397.5 38.5 all-gather.6
  439.3 106.6 all-reduce.5
  551.5 32.1 reduce-scatter.2
  585.3 34.9 all-gather.8
  627.5 187.0 all-reduce.7
  817.2 42.0 reduce-scatter.4
  861.5 40.6 all-gather.10
  959.1 108.2 all-reduce.9
where the time goes:
time: 1100 us; the launch traced here: 1090 us
  waiting for transfers between devices  611 us (56%)
  other arithmetic  371 us (34%)
  local copies, waits for them, and re-layouts  53.8 us (5%)
  matrix products  37.8 us (3%)
  between operations  17.4 us (2%)
    psum x3, waiting for transfers between devices, spread(): return lax.psum(kept, axis)  394 us
    another operation x16, other arithmetic, local(): factors = jnp.linalg.cholesky(gathered[0])  154 us
    another operation x6, other arithmetic, solve_rows(): lax.linalg.triangular_solve(factor, columns, left_side=False, lower=True,...  119 us
    all_gather x1, waiting for transfers between devices, local(): lax.all_gather(fronts.astype(jnp.bfloat16), ('row', 'col'), axis=3, tiled...  116 us
    another operation x15, other arithmetic, local(): pivot_chol = jnp.linalg.cholesky(pivot_block)  79.2 us
    all_gather x1, waiting for transfers between devices, local(): row_side = lax.all_gather(scaled, 'col', axis=0, tiled=True)  38.6 us
    reduce_scatter x1, waiting for transfers between devices, local(): lax.psum_scatter(update.astype(jnp.bfloat16), 'layer', scatter_dimension=...  32.3 us
    all_gather x1, waiting for transfers between devices, local(): lax.all_gather(shared.astype(jnp.bfloat16), 'layer', axis=0, tiled=True)  29.9 us
  transfers between devices with their start and end apart: 9, of which 7 were waited for; matrix products, arithmetic and copies ran while one was open for 14% of the time, Pallas kernels for 0%

commit v1 on v0

--- a/solution.py
+++ b/solution.py
@@ -9,9 +9,15 @@
 NP = 2
 
 
+def summed_here(x, mesh_axis):
+    parts = lax.all_gather(x, mesh_axis, axis=0, tiled=False)
+    total = parts.sum(axis=0)
+    return total
+
+
 def spread(value, axis, source):
     kept = jnp.where(lax.axis_index(axis) == source, value, 0).astype(value.dtype)
-    return lax.psum(kept, axis)
+    return summed_here(kept, axis)
 
 
 def filled_up(lines, size):

time: 1100 us -> 1820 us (1.65)
  waiting for transfers between devices: 611 us -> 1280 us
  other arithmetic: 371 us -> 415 us
    all_gather x0 -> x3, waiting for transfers between devices: none -> 1010 us  [summed_here(): parts = lax.all_gather(x, mesh_axis, axis=0, tiled=False)]
    psum x3 -> x0, waiting for transfers between devices: 394 us -> none  [spread(): return lax.psum(kept, axis)]
    reduce_sum x0 -> x3, other arithmetic: none -> 42.4 us  [summed_here(): total = parts.sum(axis=0)]
    reduce_scatter x1, waiting for transfers between devices: 0.02 us -> 40.7 us  [spread_2(): own = lax.psum_scatter(padded, axis, scatter_dimension=0, tiled=True)]
    another operation x6 -> x7, other arithmetic: 119 us -> 119 us  [solve_rows(): lax.linalg.triangular_solve(factor, columns, left_side=False, lower=True,...]
  transfers between devices with their start and end apart: 9 -> 9, of which waited for: 7 -> 8; matrix products, arithmetic and copies ran while one was open for 14% -> 9% of each run, Pallas kernels for 0% -> 0%
where the time goes in v1:
time: 1820 us; the launch traced here: 1810 us
  waiting for transfers between devices  1280 us (70%)
  other arithmetic  415 us (23%)
  local copies, waits for them, and re-layouts  57.5 us (3%)
  matrix products  39.8 us (2%)
    all_gather x3, waiting for transfers between devices, summed_here(): parts = lax.all_gather(x, mesh_axis, axis=0, tiled=False)  1010 us
    another operation x16, other arithmetic, local(): factors = jnp.linalg.cholesky(gathered[0])  154 us
    another operation x7, other arithmetic, solve_rows(): lax.linalg.triangular_solve(factor, columns, left_side=False, lower=True,...  119 us
    all_gather x1, waiting for transfers between devices, local(): lax.all_gather(fronts.astype(jnp.bfloat16), ('row', 'col'), axis=3, tiled...  116 us
    another operation x15, other arithmetic, local(): pivot_chol = jnp.linalg.cholesky(pivot_block)  79.2 us
    reduce_sum x3, other arithmetic, summed_here(): total = parts.sum(axis=0)  42.4 us
    reduce_scatter x1, waiting for transfers between devices, spread_2(): own = lax.psum_scatter(padded, axis, scatter_dimension=0, tiled=True)  40.7 us
    all_gather x1, waiting for transfers between devices, local(): row_side = lax.all_gather(scaled, 'col', axis=0, tiled=True)  38.6 us
  transfers between devices with their start and end apart: 9, of which 8 were waited for; matrix products, arithmetic and copies ran while one was open for 9% of the time, Pallas kernels for 0%

profile of v1, /device:TPU:1, one launch (start us, length us, event | category | flops | bytes accessed | tf_op | source)
XLA Modules:
  0.0 1806.7 jit_solution(2040932722426375523)
XLA Ops:
  11.6 116.1 %all-gather.10.cloned.1.call-done = bf16[1,2,512,512]{2,3,1,0:T(8,128)(2,1)} async-done(((bf16[1,2,512,8]{2,3,1,0:T(8,128)(2,1)}), bf16[1,2,512,512]{2,3,1,0:T(8,128)(2,1)}) %all-gather.10.cloned.1.call-update) | async-done | bytes 1048592 | tf_op jit(solution)/shard_map/all_gather | solution.py:59
  134.3 23.5 %custom-call.64 = f32[2,128,128]{2,1,0:T(8,128)S(1)} custom-call(f32[2,128,128]{2,1,0:T(8,128)S(1)} %cholesky.531), custom_call_target="Cholesky" | custom-call | tf_op jit(solution)/shard_map/jit(cholesky)/cholesky | solution.py:62
  157.8 19.7 %custom-call.65 = f32[2,1,128,128]{2,3,1,0:T(8,128)S(1)} custom-call(f32[2,1,128,128]{3,2,1,0:T(8,128)S(1)} %select_bitcast_fusion.2), custom_call_target="InvertDiagBlocksLowerTriangular" | custom-call | tf_op jit(solution)/shard_map/jit(cholesky)/cholesky | solution.py:62
  180.7 23.5 %custom-call.66 = f32[2,128,128]{2,1,0:T(8,128)S(1)} custom-call(f32[2,128,128]{2,1,0:T(8,128)S(1)} %cholesky.535), custom_call_target="Cholesky" | custom-call | tf_op jit(solution)/shard_map/jit(cholesky)/cholesky | solution.py:62
  204.2 19.8 %custom-call.67 = f32[2,1,128,128]{2,3,1,0:T(8,128)S(1)} custom-call(f32[2,1,128,128]{3,2,1,0:T(8,128)S(1)} %get-tuple-element.73), custom_call_target="InvertDiagBlocksLowerTriangular" | custom-call | tf_op jit(solution)/shard_map/jit(cholesky)/cholesky | solution.py:62
  226.1 23.5 %custom-call.68 = f32[2,128,128]{2,1,0:T(8,128)S(1)} custom-call(f32[2,128,128]{2,1,0:T(8,128)S(1)} %cholesky.540), custom_call_target="Cholesky" | custom-call | tf_op jit(solution)/shard_map/jit(cholesky)/cholesky | solution.py:62
  249.5 19.7 %custom-call.69 = f32[2,1,128,128]{2,3,1,0:T(8,128)S(1)} custom-call(f32[2,1,128,128]{3,2,1,0:T(8,128)S(1)} %get-tuple-element.71), custom_call_target="InvertDiagBlocksLowerTriangular" | custom-call | tf_op jit(solution)/shard_map/jit(cholesky)/cholesky | solution.py:62
  271.0 23.7 %custom-call.70 = f32[2,128,128]{2,1,0:T(8,128)S(1)} custom-call(f32[2,128,128]{2,1,0:T(8,128)S(1)} %convolution_subtract_fusion.7), custom_call_target="Cholesky" | custom-call | tf_op jit(solution)/shard_map/jit(cholesky)/cholesky | solution.py:62
  304.2 39.3 %custom-call.78 = f32[4,128,128]{1,2,0:T(8,128)S(1)} custom-call(f32[4,128,128]{2,1,0:T(8,128)S(1)} %get-tuple-element.26), custom_call_target="InvertDiagBlocksLowerTriangular" | custom-call | tf_op jit(solution)/shard_map/triangular_solve/custom-call.14 | solution.py:47
  354.0 39.7 %custom-call.79 = f32[4,128,128]{1,2,0:T(8,128)S(1)} custom-call(f32[4,128,128]{2,1,0:T(8,128)S(1)} %get-tuple-element.27), custom_call_target="InvertDiagBlocksLowerTriangular" | custom-call | tf_op jit(solution)/shard_map/triangular_solve/custom-call.14 | solution.py:47
  397.0 38.6 %all-gather.12.cloned.1.call-done = bf16[1024,1024]{0,1:T(8,128)(2,1)} async-done(((bf16[128,1024]{0,1:T(8,128)(2,1)}), bf16[1024,1024]{0,1:T(8,128)(2,1)}) %all-gather.12.cloned.1.call-update) | async-done | bytes 2097168 | tf_op jit(solution)/shard_map/all_gather | solution.py:77
  437.1 326.6 %all-gather.20.cloned.1.call-done = bf16[8192,1024]{0,1:T(8,128)(2,1)} async-done(((bf16[1024,1024]{0,1:T(8,128)(2,1)}), bf16[8192,1024]{0,1:T(8,128)(2,1)}) %all-gather.20.cloned.1.call-update) | async-done | bytes 16777232 | tf_op jit(solution)/shard_map/all_gather | solution.py:13
  763.7 15.6 copy.75
  794.7 33.4 %reduce-scatter.3.cloned.1.call-done = bf16[256,1024]{1,0:T(8,128)(2,1)} async-done(((bf16[1024,1024]{1,0:T(8,128)(2,1)}), bf16[256,1024]{1,0:T(8,128)(2,1)}) %reduce-scatter.3.cloned.1.call-update) | async-done | bytes 524304 | tf_op jit(solution)/shard_map/reduce_scatter | solution.py:82
  828.2 34.6 %all-gather.14.cloned.1.call-done = bf16[1024,1024]{1,0:T(8,128)(2,1)} async-done(((bf16[256,1024]{1,0:T(8,128)(2,1)}), bf16[1024,1024]{1,0:T(8,128)(2,1)}) %all-gather.14.cloned.1.call-update) | async-done | bytes 2097168 | tf_op jit(solution)/shard_map/all_gather | solution.py:85
  870.0 40.7 %reduce-scatter.5.cloned.1.call-done = f32[128,512]{1,0:T(8,128)} async-done(((f32[1024,512]{1,0:T(8,128)}), f32[128,512]{1,0:T(8,128)}) %reduce-scatter.5.cloned.1.call-update) | async-done | bytes 262160 | tf_op jit(solution)/shard_map/reduce_scatter | solution.py:33
  910.8 367.9 %all-gather.22.cloned.1.call-done = f32[32768,512]{1,0:T(8,128)} async-done(((f32[512,512]{1,0:T(8,128)}), f32[32768,512]{1,0:T(8,128)}) %all-gather.22.cloned.1.call-update) | async-done | bytes 67108880 | tf_op jit(solution)/shard_map/all_gather | solution.py:13
  1278.7 21.4 %reduce_sum.31 = f32[512,512]{1,0:T(8,128)S(1)} reduce(f32[64,512,512]{2,1,0:T(8,128)} %bitcast.29, f32[]{:T(128)} %constant.333.clone.1), dimensions={0}, to_apply=%region_11.13 | reduce | flops 16515072 | bytes 68157440 | tf_op jit(solution)/shard_map/reduce_sum | solution.py:14
  1300.7 11.7 cholesky.467
  1323.0 11.7 cholesky.483
  1345.4 11.7 cholesky.504
  1367.6 11.7 cholesky.521
  1393.4 39.3 %custom-call.74 = f32[4,128,128]{1,2,0:T(8,128)S(1)} custom-call(f32[4,128,128]{2,1,0:T(8,128)S(1)} %get-tuple-element.19), custom_call_target="InvertDiagBlocksLowerTriangular" | custom-call | tf_op jit(solution)/shard_map/triangular_solve | solution.py:47
  1459.3 317.9 %all-gather.18.cloned.1.call-done = f32[8,1024,512]{2,1,0:T(8,128)} async-done(((f32[1,1024,512]{2,1,0:T(8,128)}), f32[8,1024,512]{2,1,0:T(8,128)}) %all-gather.18.cloned.1.call-update) | async-done | bytes 16777232 | tf_op jit(solution)/shard_map/all_gather | solution.py:13
  (190 shorter events, 182.4 us)
Async XLA Ops:
  7.2 120.6 %all-gather.10.cloned.1.call-start = ((), (), s32[]{:S(2)}) async-start(), calls=%async_computation.2 | async-start | bytes 1064960 | tf_op jit(solution)/shard_map/all_gather | solution.py:59
  8.6 427.0 %all-gather.12.cloned.1.call-start = ((), (), s32[]{:S(2)}) async-start(), calls=%async_computation.3 | async-start | bytes 2359296 | tf_op jit(solution)/shard_map/all_gather | solution.py:77
  130.6 2.0 copy-start.5
  132.9 1.3 copy-start.4
  295.4 48.1 %copy-start.12 = (f32[128,512]{1,0:T(8,128)S(1)}, f32[128,512]{1,0:T(8,128)}, u32[]{:S(2)}) copy-start(f32[128,512]{1,0:T(8,128)} %get-tuple-element.68) | copy-start | bytes 786436
  295.7 98.0 %copy-start.11 = (f32[128,512]{1,0:T(8,128)S(1)}, f32[128,512]{1,0:T(8,128)}, u32[]{:S(2)}) copy-start(f32[128,512]{1,0:T(8,128)} %get-tuple-element.69) | copy-start | bytes 786436
  396.9 366.8 %all-gather.20.cloned.1.call-start = ((), (), s32[]{:S(2)}) async-start(), calls=%async_computation.9 | async-start | bytes 18874368 | tf_op jit(solution)/shard_map/all_gather | solution.py:13
  437.1 391.1 %reduce-scatter.3.cloned.1.call-start = ((), (), s32[]{:S(2)}) async-start(), calls=%async_computation.4 | async-start | bytes 2621440 | tf_op jit(solution)/shard_map/reduce_scatter | solution.py:82
  779.4 11.6 copy-start.10
  794.7 68.1 %all-gather.14.cloned.1.call-start = ((), (), s32[]{:S(2)}) async-start(), calls=%async_computation.5 | async-start | bytes 2621440 | tf_op jit(solution)/shard_map/all_gather | solution.py:85
  828.2 82.6 %reduce-scatter.5.cloned.1.call-start = ((), (), s32[]{:S(2)}) async-start(), calls=%async_computation.6 | async-start | bytes 2359296 | tf_op jit(solution)/shard_map/reduce_scatter | solution.py:33
  862.8 2.8 copy-start.6
  865.6 2.6 copy-start
  868.3 1.7 copy-start.2
  868.3 410.4 %all-gather.22.cloned.1.call-start = ((), (), s32[]{:S(2)}) async-start(), calls=%async_computation.10 | async-start | bytes 68157440 | tf_op jit(solution)/shard_map/all_gather | solution.py:13
  870.0 562.8 %all-gather.16.cloned.1.call-start = ((), (), s32[]{:S(2)}) async-start(), calls=%async_computation.7 | async-start | bytes 2359296 | tf_op jit(solution)/shard_map/all_gather | solution.py:34
  910.8 866.4 %all-gather.18.cloned.1.call-start = ((), (), s32[]{:S(2)}) async-start(), calls=%async_computation.8 | async-start | bytes 18874368 | tf_op jit(solution)/shard_map/all_gather | solution.py:13
  1393.4 43.9 %copy-start.7 = (f32[512,512]{1,0:T(8,128)}, f32[512,512]{1,0:T(8,128)S(1)}, u32[]{:S(2)}) copy-start(f32[512,512]{1,0:T(8,128)S(1)} %get-tuple-element.248) | copy-start | bytes 3145732
  1432.8 4.5 copy-start.9
  1449.8 7.3 copy-start.8
  1786.6 5.6 copy-start.1
  1786.6 5.6 copy-start.3
Sparse Core Ops, SparseCore 0:
  10.4 117.2 all-gather.9
  397.0 38.5 all-gather.11
  438.0 325.7 all-gather.19
  794.8 33.2 reduce-scatter.2
  829.8 32.9 all-gather.13
  868.4 42.2 reduce-scatter.4
  912.6 366.0 all-gather.21
  1280.6 36.9 all-gather.15
  1448.8 328.3 all-gather.17
